TPU v7x, 32 devices: a whole 2x2x4 slice. The times are simulated.
32 devices in a mesh: fsdp: 8 (over y, x, core), tp: 4 (over z).
Axes of the slice: x: 2, y: 2, z: 4, core: 2. Of those that a mesh axis runs over, the one named last changes fastest.
Arguments:
- inputs: float32 [8192, 768], P(('fsdp', 'tp')), may hold values from -6 to 6
- out_cotangent: float32 [8192, 768], P('fsdp'), may hold values from -6 to 6
- clip_lengths: int32 [6], replicated, may hold values from 384 to 1536, as said below
- norm1_gain: float32 [768], replicated, may hold values from 0.5 to 1.5
- norm1_shift: float32 [768], replicated, may hold values from -3 to 3
- query_weight: bfloat16 [768, 768], P('fsdp', 'tp'), may hold values from -0.21875 to 0.21875
- query_bias: float32 [768], replicated, may hold values from -3 to 3
- key_weight: bfloat16 [768, 768], P('fsdp', 'tp'), may hold values from -0.21875 to 0.21875
- value_weight: bfloat16 [768, 768], P('fsdp', 'tp'), may hold values from -0.21875 to 0.21875
- value_bias: float32 [768], replicated, may hold values from -3 to 3
- out_weight: bfloat16 [768, 768], P('fsdp', 'tp'), may hold values from -0.75 to 0.75
- out_bias: float32 [768], replicated, may hold values from -3 to 3
- norm2_gain: float32 [768], replicated, may hold values from 0.5 to 1.5
- norm2_shift: float32 [768], replicated, may hold values from -3 to 3
- fc1_weight: bfloat16 [3072, 768], P(('fsdp', 'tp')), may hold values from -0.21875 to 0.21875
- fc1_bias: float32 [3072], replicated, may hold values from -3 to 3
- fc2_weight: bfloat16 [3072, 768], P(('fsdp', 'tp')), may hold values from -0.3125 to 0.3125
- fc2_bias: float32 [768], replicated, may hold values from -3 to 3
Outputs:
- outputs: float32 [8192, 768], P(('fsdp', 'tp'))
- inputs_grad: float32 [8192, 768], P(('fsdp', 'tp'))
- norm1_gain_grad: float32 [768], replicated
- norm1_shift_grad: float32 [768], replicated
- query_weight_grad: float32 [768, 768], P('fsdp', 'tp')
- query_bias_grad: float32 [768], replicated
- key_weight_grad: float32 [768, 768], P('fsdp', 'tp')
- value_weight_grad: float32 [768, 768], P('fsdp', 'tp')
- value_bias_grad: float32 [768], replicated
- out_weight_grad: float32 [768, 768], P('fsdp', 'tp')
- out_bias_grad: float32 [768], replicated
- norm2_gain_grad: float32 [768], replicated
- norm2_shift_grad: float32 [768], replicated
- fc1_weight_grad: float32 [3072, 768], P(('fsdp', 'tp'))
- fc1_bias_grad: float32 [3072], replicated
- fc2_weight_grad: float32 [3072, 768], P(('fsdp', 'tp'))
- fc2_bias_grad: float32 [768], replicated
Inputs may be any that keep to these rules, and one draw needn't show every extreme that they name: `clip_lengths`: clip c has at most min(1536, 8192 - c * 1536) valid frames; some clip has all 1536 frames valid.
All inputs are finite; a program needn't handle non-finite values.
Results may differ from a plain program's by a relative error of at most 0.03.
Values may be sent and summed in bfloat16 or wider, within the bound.
A program may use at most 128 MiB of HBM per device.

v0:
```python
import math
import jax
import jax.numpy as jnp
from jax import lax
from jax.sharding import PartitionSpec as P

HD = 64
CLIP = 1536
QB = 512
eps_norm = 1e-05
root_half = 0.7071067811865476
inv_root_tau = 0.3989422804014327
far_negative = -1e30


def extended(value, sides, width):
    for axis, dim in sides:
        size, length = (lax.axis_size(axis), value.shape[dim])
        up = [(i, (i + 1) % size) for i in range(size - 1)]
        down = [(j, i) for i, j in up]
        last = lax.slice_in_dim(value, length - width, length, axis=dim)
        initial = lax.slice_in_dim(value, 0, width, axis=dim)
        before = lax.ppermute(last, axis, up)
        after = lax.ppermute(initial, axis, down)
        value = jnp.concatenate([before, value, after], axis=dim)
    return value


def normalize(rows, gain, shift):
    centre = jnp.mean(rows, axis=-1, keepdims=True)
    centred = rows - centre
    inv_spread = lax.rsqrt(jnp.mean(centred * centred, axis=-1, keepdims=True) + eps_norm)
    unit_rows = centred * inv_spread
    return (unit_rows, inv_spread, unit_rows * gain + shift)


def norm_back(upstream, unit_rows, inv_spread, gain):
    scaled = upstream * gain
    return inv_spread * (
        scaled
        - jnp.mean(scaled, axis=-1, keepdims=True)
        - unit_rows * jnp.mean(scaled * unit_rows, axis=-1, keepdims=True)
    )


def gelu_exact(values):
    return 0.5 * values * (1.0 + lax.erf(values * root_half))


def gelu_slope(values):
    return (
        0.5 * (1.0 + lax.erf(values * root_half))
        + values * jnp.exp(-0.5 * values * values) * inv_root_tau
    )


def contract_rows(left_rows, right_rows):
    return lax.dot_general(
        left_rows, right_rows, (((0,), (0,)), ((), ())), preferred_element_type=jnp.float32
    )


def contract_cols(left_rows, right_rows):
    return lax.dot_general(
        left_rows, right_rows, (((1,), (1,)), ((), ())), preferred_element_type=jnp.float32
    )


def fetch_attention(query_weight, key_weight, value_weight, out_weight):
    return (
        lax.all_gather(query_weight, "fsdp", axis=0, tiled=True),
        lax.all_gather(key_weight, "fsdp", axis=0, tiled=True),
        lax.all_gather(value_weight, "fsdp", axis=0, tiled=True),
        lax.all_gather(out_weight, "fsdp", axis=0, tiled=True),
    )


def on_device(
    inputs,
    out_cotangent,
    clip_lengths,
    norm1_gain,
    norm1_shift,
    query_weight,
    query_bias,
    key_weight,
    value_weight,
    value_bias,
    out_weight,
    out_bias,
    norm2_gain,
    norm2_shift,
    fc1_weight,
    fc1_bias,
    fc2_weight,
    fc2_bias,
):
    bf16 = jnp.bfloat16
    f32 = jnp.float32
    tp_count = lax.axis_size("tp")
    fsdp_count = lax.axis_size("fsdp")
    tp_index = lax.axis_index("tp")
    fsdp_index = lax.axis_index("fsdp")
    own_rows = inputs.shape[0]
    group_rows = out_cotangent.shape[0]
    score_scale = 1.0 / math.sqrt(HD)
    margin = CLIP - QB
    tp_slot = (jnp.arange(tp_count) == tp_index).astype(f32)
    own_cotangent = lax.dynamic_slice_in_dim(out_cotangent, tp_index * own_rows, own_rows, 0)
    unit1, spread1, normed_own = normalize(inputs, norm1_gain, norm1_shift)
    normed = lax.all_gather(normed_own.astype(bf16), "tp", axis=0, tiled=True)
    query_w, key_w, value_w, out_w = fetch_attention(
        query_weight, key_weight, value_weight, out_weight
    )
    local_width = query_w.shape[1]
    heads_here = local_width // HD
    column_start = tp_index * local_width
    query = (
        jnp.dot(normed, query_w, preferred_element_type=f32)
        + lax.dynamic_slice_in_dim(query_bias, column_start, local_width, 0)
    ).astype(bf16)
    key = jnp.dot(normed, key_w, preferred_element_type=f32).astype(bf16)
    value = (
        jnp.dot(normed, value_w, preferred_element_type=f32)
        + lax.dynamic_slice_in_dim(value_bias, column_start, local_width, 0)
    ).astype(bf16)
    padded = extended(jnp.stack([key, value]), (("fsdp", 1),), margin)
    group_base = fsdp_index * group_rows
    clip_ids = jnp.arange(clip_lengths.shape[0])
    block_count = group_rows // QB

    def block_scores(block_index):
        first_row = block_index * QB
        clip_index = (group_base + first_row) // CLIP
        key_start = clip_index * CLIP - group_base + margin
        length = jnp.sum(jnp.where(clip_ids == clip_index, clip_lengths, 0))
        query_block = lax.dynamic_slice_in_dim(query, first_row, QB, 0).reshape(QB, heads_here, HD)
        pair = lax.dynamic_slice_in_dim(padded, key_start, CLIP, 1).reshape(2, CLIP, heads_here, HD)
        scores = (
            jnp.einsum("qhe,khe->hqk", query_block, pair[0], preferred_element_type=f32)
            * score_scale
        )
        scores = jnp.where((jnp.arange(CLIP) < length)[None, None, :], scores, far_negative)
        return (first_row, key_start, query_block, pair[0], pair[1], scores)

    def attend(block_index, carry):
        context_rows, total_rows = carry
        first_row, key_start, query_block, key_block, value_block, scores = block_scores(
            block_index
        )
        highest = jnp.max(scores, axis=-1, keepdims=True)
        log_total = highest[..., 0] + jnp.log(jnp.sum(jnp.exp(scores - highest), axis=-1))
        weights = jnp.exp(scores - log_total[..., None]).astype(bf16)
        block_out = jnp.einsum("hqk,khe->qhe", weights, value_block, preferred_element_type=f32)
        block_out = block_out.astype(bf16).reshape(QB, local_width)
        context_rows = lax.dynamic_update_slice_in_dim(context_rows, block_out, first_row, 0)
        total_rows = lax.dynamic_update_slice_in_dim(total_rows, log_total, first_row, 1)
        return (context_rows, total_rows)

    context, totals = lax.fori_loop(
        0,
        block_count,
        attend,
        (jnp.zeros((group_rows, local_width), bf16), jnp.zeros((heads_here, group_rows), f32)),
    )
    attended = lax.psum_scatter(
        contract_cols(context, out_w), "tp", scatter_dimension=0, tiled=True
    )
    hidden = inputs + attended + out_bias
    unit2, spread2, normed2_full = normalize(hidden, norm2_gain, norm2_shift)
    normed2_own = normed2_full.astype(bf16)
    normed2 = lax.all_gather(normed2_own, "tp", axis=0, tiled=True)
    w_up, w_down = (
        lax.all_gather(fc1_weight, "fsdp", axis=0, tiled=True),
        lax.all_gather(fc2_weight, "fsdp", axis=0, tiled=True),
    )
    unit_count = fc1_weight.shape[0]
    bias_up = lax.dynamic_index_in_dim(
        fc1_bias.reshape(fsdp_count, tp_count, unit_count), tp_index, 1, False
    ).reshape(-1)
    preact = contract_cols(normed2, w_up) + bias_up
    activated = gelu_exact(preact).astype(bf16)
    mixed = lax.psum_scatter(
        jnp.dot(activated, w_down, preferred_element_type=f32),
        "tp",
        scatter_dimension=0,
        tiled=True,
    )
    outputs = hidden + mixed + fc2_bias
    up_rounded = out_cotangent.astype(bf16)
    dactivated = contract_cols(up_rounded, w_down)
    dpreact = (dactivated * gelu_slope(preact)).astype(bf16)
    grad_up_part = contract_rows(dpreact, normed2)
    grad_down_part = contract_rows(activated, up_rounded)
    upbias_part = jnp.sum(dpreact.astype(f32), axis=0)
    grad_b1 = (upbias_part.reshape(fsdp_count, 1, unit_count) * tp_slot[None, :, None]).reshape(-1)
    dnorm2 = lax.psum_scatter(
        jnp.dot(dpreact, w_up, preferred_element_type=f32), "tp", scatter_dimension=0, tiled=True
    )
    grad_fc1, grad_fc2 = (
        lax.psum_scatter(grad_up_part, "fsdp", scatter_dimension=0, tiled=True),
        lax.psum_scatter(grad_down_part, "fsdp", scatter_dimension=0, tiled=True),
    )
    grad_b2 = jnp.sum(own_cotangent, axis=0)
    grad_gain2 = jnp.sum(dnorm2 * unit2, axis=0)
    grad_shift2 = jnp.sum(dnorm2, axis=0)
    dhidden = own_cotangent + norm_back(dnorm2, unit2, spread2, norm2_gain)
    grad_obias = jnp.sum(dhidden, axis=0)
    query_w, key_w, value_w, out_w = fetch_attention(
        query_weight, key_weight, value_weight, out_weight
    )
    dh_all = lax.all_gather(dhidden.astype(bf16), "tp", axis=0, tiled=True)
    dcontext = jnp.dot(dh_all, out_w, preferred_element_type=f32).astype(bf16)
    grad_out = contract_rows(dh_all, context)
    delta = jnp.sum(
        (dcontext.astype(f32) * context.astype(f32)).reshape(group_rows, heads_here, HD), axis=-1
    ).T

    def attend_back(block_index, carry):
        dquery_rows, dpair = carry
        first_row, key_start, query_block, key_block, value_block, scores = block_scores(
            block_index
        )
        grad_block = lax.dynamic_slice_in_dim(dcontext, first_row, QB, 0).reshape(
            QB, heads_here, HD
        )
        probs = jnp.exp(scores - lax.dynamic_slice_in_dim(totals, first_row, QB, 1)[..., None])
        delta_block = lax.dynamic_slice_in_dim(delta, first_row, QB, 1)
        dprobs = jnp.einsum("qhe,khe->hqk", grad_block, value_block, preferred_element_type=f32)
        dscores = (probs * (dprobs - delta_block[..., None]) * score_scale).astype(bf16)
        dquery_block = jnp.einsum("hqk,khe->qhe", dscores, key_block, preferred_element_type=f32)
        dquery_block = dquery_block.astype(bf16).reshape(QB, local_width)
        dkey_block = jnp.einsum(
            "hqk,qhe->khe", dscores, query_block, preferred_element_type=f32
        ).reshape(CLIP, local_width)
        dvalue_block = jnp.einsum(
            "hqk,qhe->khe", probs.astype(bf16), grad_block, preferred_element_type=f32
        ).reshape(CLIP, local_width)
        current = lax.dynamic_slice_in_dim(dpair, key_start, CLIP, 1)
        dpair = lax.dynamic_update_slice_in_dim(
            dpair, current + jnp.stack([dkey_block, dvalue_block]), key_start, 1
        )
        dquery_rows = lax.dynamic_update_slice_in_dim(dquery_rows, dquery_block, first_row, 0)
        return (dquery_rows, dpair)

    dquery, dpair = lax.fori_loop(
        0,
        block_count,
        attend_back,
        (jnp.zeros((group_rows, local_width), bf16), jnp.zeros(padded.shape, f32)),
    )
    rims = jnp.concatenate([dpair[:, :margin], dpair[:, margin + group_rows :]], axis=1)
    received = extended(rims, (("fsdp", 1),), margin)
    inner_part = dpair[:, margin : margin + group_rows]
    inner_part = inner_part.at[:, :margin].add(received[:, :margin])
    inner_part = inner_part.at[:, group_rows - margin :].add(received[:, 3 * margin :])
    dkey = inner_part[0].astype(bf16)
    dvalue = inner_part[1].astype(bf16)
    grad_query = contract_rows(normed, dquery)
    grad_key = contract_rows(normed, dkey)
    grad_value = contract_rows(normed, dvalue)
    grad_qbias = (tp_slot[:, None] * jnp.sum(dquery.astype(f32), axis=0)[None, :]).reshape(-1)
    grad_vbias = (tp_slot[:, None] * jnp.sum(dvalue.astype(f32), axis=0)[None, :]).reshape(-1)
    dnorm1 = lax.psum_scatter(
        contract_cols(dquery, query_w)
        + contract_cols(dkey, key_w)
        + contract_cols(dvalue, value_w),
        "tp",
        scatter_dimension=0,
        tiled=True,
    )
    grad_gain1 = jnp.sum(dnorm1 * unit1, axis=0)
    grad_shift1 = jnp.sum(dnorm1, axis=0)
    inputs_grad = dhidden + norm_back(dnorm1, unit1, spread1, norm1_gain)
    grad_query, grad_key, grad_value, grad_out = (
        lax.psum_scatter(grad_query, "fsdp", scatter_dimension=0, tiled=True),
        lax.psum_scatter(grad_key, "fsdp", scatter_dimension=0, tiled=True),
        lax.psum_scatter(grad_value, "fsdp", scatter_dimension=0, tiled=True),
        lax.psum_scatter(grad_out, "fsdp", scatter_dimension=0, tiled=True),
    )
    (
        grad_gain1,
        grad_shift1,
        grad_qbias,
        grad_vbias,
        grad_obias,
        grad_gain2,
        grad_shift2,
        grad_b1,
        grad_b2,
    ) = lax.psum(
        (
            grad_gain1,
            grad_shift1,
            grad_qbias,
            grad_vbias,
            grad_obias,
            grad_gain2,
            grad_shift2,
            grad_b1,
            grad_b2,
        ),
        ("fsdp", "tp"),
    )
    return (
        outputs,
        inputs_grad,
        grad_gain1,
        grad_shift1,
        grad_query,
        grad_qbias,
        grad_key,
        grad_value,
        grad_vbias,
        grad_out,
        grad_obias,
        grad_gain2,
        grad_shift2,
        grad_fc1,
        grad_b1,
        grad_fc2,
        grad_b2,
    )


def solution(mesh):
    in_specs = (
        P(("fsdp", "tp"), None),
        P("fsdp", None),
        P(),
        P(),
        P(),
        P("fsdp", "tp"),
        P(),
        P("fsdp", "tp"),
        P("fsdp", "tp"),
        P(),
        P("fsdp", "tp"),
        P(),
        P(),
        P(),
        P(("fsdp", "tp"), None),
        P(),
        P(("fsdp", "tp"), None),
        P(),
    )
    out_specs = (
        P(("fsdp", "tp"), None),
        P(("fsdp", "tp"), None),
        P(),
        P(),
        P("fsdp", "tp"),
        P(),
        P("fsdp", "tp"),
        P("fsdp", "tp"),
        P(),
        P("fsdp", "tp"),
        P(),
        P(),
        P(),
        P(("fsdp", "tp"), None),
        P(),
        P(("fsdp", "tp"), None),
        P(),
    )
    return jax.shard_map(
        on_device, mesh=mesh, in_specs=in_specs, out_specs=out_specs, check_vma=False
    )
```

profile of v0, /device:TPU:0, one launch (start us, length us, event | category | flops | bytes accessed | tf_op | source)
XLA Modules:
  0.0 818.0 jit_solution(7291975622718793777)
XLA Ops:
  10.7 2.1 add_convert_fusion.2
  13.7 11.0 %all_gather.32 = bf16[768,192]{1,0:T(8,128)(2,1)S(1)} all-gather(bf16[96,192]{1,0:T(8,128)(2,1)S(1)} %copy-done.22), channel_id=1, replica_groups=mesh['fsdp'=8,'tp'=4] {'fsdp'}, dimensions={0}, use_global_device_ids=true | all-gather | bytes 331776 | tf_op jit(solution)/shard_map/all_gather | solution.py:72
  24.7 9.5 %all_gather.33 = bf16[768,192]{1,0:T(8,128)(2,1)S(1)} all-gather(bf16[96,192]{1,0:T(8,128)(2,1)S(1)} %copy-done.23), channel_id=1, replica_groups=mesh['fsdp'=8,'tp'=4] {'fsdp'}, dimensions={0}, use_global_device_ids=true | all-gather | bytes 331776 | tf_op jit(solution)/shard_map/all_gather | solution.py:73
  34.3 18.5 %all-gather.6.cloned.1.call-done = bf16[1024,768]{1,0:T(8,128)(2,1)} async-done(((bf16[256,768]{1,0:T(8,128)(2,1)}), bf16[1024,768]{1,0:T(8,128)(2,1)}) %all-gather.6.cloned.1.call-update) | async-done | bytes 1572880 | tf_op jit(solution)/shard_map/all_gather | solution.py:111
  52.8 2.2 fusion.27
  55.0 2.1 fusion.28
  59.3 4.0 collective-permute-start
  64.0 18.6 %all_gather.34 = bf16[768,192]{1,0:T(8,128)(2,1)S(1)} all-gather(bf16[96,192]{1,0:T(8,128)(2,1)S(1)} %copy-done.24), channel_id=1, replica_groups=mesh['fsdp'=8,'tp'=4] {'fsdp'}, dimensions={0}, use_global_device_ids=true | all-gather | bytes 331776 | tf_op jit(solution)/shard_map/all_gather | solution.py:71
  82.6 11.4 %all_gather.35 = bf16[768,192]{1,0:T(8,128)(2,1)} all-gather(bf16[96,192]{1,0:T(8,128)(2,1)S(1)} %copy-done.25), channel_id=1, replica_groups=mesh['fsdp'=8,'tp'=4] {'fsdp'}, dimensions={0}, use_global_device_ids=true | all-gather | bytes 331776 | tf_op jit(solution)/shard_map/all_gather | solution.py:74
  94.7 1.5 pad_maximum_fusion
  97.1 17.5 %while.40 = (s32[]{:T(128)}, bf16[1024,192]{0,1:T(8,128)(2,1)}, f32[3,1024]{1,0:T(4,128)S(1)}, s32[]{:T(128)}, bf16[2,3072,192]{1,2,0:T(8,128)(2,1)S(1)}, /*inde...) while((s32[]{:T(128)}, bf16[1024,192]{0,1:T(8,128)(2,1)}, ...), condition=%wide.region_6.7_spmd.clone, body=%wide.region_2.6_spmd.clone.sunk | while | flops 630030336 | bytes 36239832 | solution.py:160
  99.1 1.6 fusion.114
  100.7 2.1 exponential_reduce_fusion.2
  102.8 2.2 fusion.115
  107.9 1.6 fusion.114
  109.5 2.1 exponential_reduce_fusion.2
  111.6 2.2 fusion.115
  114.6 3.5 fusion.40
  118.7 58.8 %reduce-scatter.11.cloned.1.call-done = f32[256,768]{1,0:T(8,128)} async-done(((f32[1024,768]{1,0:T(8,128)}), f32[256,768]{1,0:T(8,128)}) %reduce-scatter.11.cloned.1.call-update) | async-done | bytes 786448 | tf_op jit(solution)/shard_map/reduce_scatter | solution.py:166
  181.5 1.4 reshape.289
  184.3 33.2 %all-gather.8.cloned.1.call-done = bf16[1024,768]{1,0:T(8,128)(2,1)} async-done(((bf16[256,768]{1,0:T(8,128)(2,1)}), bf16[1024,768]{1,0:T(8,128)(2,1)}) %all-gather.8.cloned.1.call-update) | async-done | bytes 1572880 | tf_op jit(solution)/shard_map/all_gather | solution.py:172
  217.6 5.4 multiply_convert_fusion.1
  223.0 19.1 %all-gather.12.cloned.1.call-done = bf16[768,768]{1,0:T(8,128)(2,1)} async-done(((bf16[96,768]{1,0:T(8,128)(2,1)}), bf16[768,768]{1,0:T(8,128)(2,1)}) %all-gather.12.cloned.1.call-update) | async-done | bytes 1179664 | tf_op jit(solution)/shard_map/all_gather | solution.py:175
  242.1 6.1 convert_reduce_fusion
  249.4 3.0 fusion.42
  252.5 4.8 fusion.41
  257.4 55.6 %reduce-scatter.15.cloned.1.call-done = f32[256,768]{1,0:T(8,128)} async-done(((f32[1024,768]{1,0:T(8,128)}), f32[256,768]{1,0:T(8,128)}) %reduce-scatter.15.cloned.1.call-update) | async-done | bytes 786448 | tf_op jit(solution)/shard_map/reduce_scatter | solution.py:197
  312.9 2.4 multiply_reduce_fusion
  315.9 59.7 %reduce-scatter.13.cloned.1.call-done = f32[256,768]{1,0:T(8,128)} async-done(((f32[1024,768]{1,0:T(8,128)}), f32[256,768]{1,0:T(8,128)}) %reduce-scatter.13.cloned.1.call-update) | async-done | bytes 786448 | tf_op jit(solution)/shard_map/reduce_scatter | solution.py:183
  375.5 3.7 fusion.35
  381.2 36.8 %all-gather.14.cloned.1.call-done = bf16[1024,768]{1,0:T(8,128)(2,1)} async-done(((bf16[256,768]{1,0:T(8,128)(2,1)}), bf16[1024,768]{1,0:T(8,128)(2,1)}) %all-gather.14.cloned.1.call-update) | async-done | bytes 1572880 | tf_op jit(solution)/shard_map/all_gather | solution.py:212
  418.0 3.3 convert_multiply_fusion
  423.2 2.7 broadcast_in_dim.131
  425.9 32.3 %while.41 = (s32[]{:T(128)}, bf16[1024,192]{0,1:T(8,128)(2,1)}, f32[2,3072,192]{1,2,0:T(8,128)}, s32[]{:T(128)}, bf16[2,3072,192]{1,2,0:T(8,128)(2,1)S(1)}, /*in...) while((s32[]{:T(128)}, bf16[1024,192]{0,1:T(8,128)(2,1)}, ...), condition=%wide.region_17.18_spmd.clone, body=%wide.region_15.17_spmd.clone.sunk | while | flops 1537181184 | bytes 94420032 | solution.py:246
  429.7 1.4 fusion.126
  431.1 2.1 fusion.128
  433.2 3.4 multiply_convert_fusion.3
  436.6 1.5 convolution_convert_fusion.4
  440.0 2.1 copy-done
  445.8 1.4 fusion.126
  447.2 2.1 fusion.128
  449.3 3.4 multiply_convert_fusion.3
  452.8 1.5 convolution_convert_fusion.4
  456.1 2.1 copy-done
  458.2 2.2 fusion.37
  460.4 1.4 collective-permute-start.2
  464.7 4.0 collective-permute-done.3
  468.7 1.8 add_convert_fusion
  471.8 2.3 add_add_fusion
  475.5 4.3 fusion.46
  480.2 5.2 fusion.29
  485.5 3.0 fusion.45
  488.6 1.6 fusion.44
  491.4 1.6 fusion.32
  496.9 2.5 fusion.34
  499.4 63.9 %reduce-scatter.17.cloned.1.call-done = f32[256,768]{1,0:T(8,128)} async-done(((f32[1024,768]{1,0:T(8,128)}), f32[256,768]{1,0:T(8,128)}) %reduce-scatter.17.cloned.1.call-update) | async-done | bytes 786448 | tf_op jit(solution)/shard_map/reduce_scatter | solution.py:264
  563.3 1.5 multiply_reduce_fusion.1
  564.9 41.5 %all-reduce = (f32[768]{0:T(1024)}, f32[768]{0:T(1024)}, f32[768]{0:T(1024)}, f32[768]{0:T(1024)}, f32[768]{0:T(1024)}, /*index=5*/f32[768]{0:T(1024)}, f32[768]{0:T(1024)}, f32[3072]{0:T(1024)}, f32[768]{0:T(1024)}) all-reduce(f32[768]{0:T(1024)S(1)} %get-tuple-element.569, ...), channel_id=1, replica_groups=mesh['fsdp'=8,'tp'=4] {'fsdp','tp'}, use_global_device_ids=true, to_apply=%region_22.23 | all-reduce | flops 9216 | bytes 73728 | tf_op jit(solution)/shard_map/psum | solution.py:291
  606.4 2.3 multiply_add_fusion
  609.5 46.3 %reduce-scatter.29.cloned.1.call-done = f32[96,768]{1,0:T(8,128)} async-done(((f32[768,768]{1,0:T(8,128)}), f32[96,768]{1,0:T(8,128)}) %reduce-scatter.29.cloned.1.call-update) | async-done | bytes 294928 | tf_op jit(solution)/shard_map/reduce_scatter | solution.py:202
  655.8 38.7 %reduce-scatter.25.cloned.1.call-done = f32[96,192]{1,0:T(8,128)} async-done(((f32[768,192]{1,0:T(8,128)}), f32[96,192]{1,0:T(8,128)}) %reduce-scatter.25.cloned.1.call-update) | async-done | bytes 73744 | tf_op jit(solution)/shard_map/reduce_scatter | solution.py:279
  694.5 38.7 %reduce-scatter.19.cloned.1.call-done = f32[96,192]{1,0:T(8,128)} async-done(((f32[768,192]{1,0:T(8,128)}), f32[96,192]{1,0:T(8,128)}) %reduce-scatter.19.cloned.1.call-update) | async-done | bytes 73744 | tf_op jit(solution)/shard_map/reduce_scatter | solution.py:276
  733.2 38.7 %reduce-scatter.21.cloned.1.call-done = f32[96,192]{1,0:T(8,128)} async-done(((f32[768,192]{1,0:T(8,128)}), f32[96,192]{1,0:T(8,128)}) %reduce-scatter.21.cloned.1.call-update) | async-done | bytes 73744 | tf_op jit(solution)/shard_map/reduce_scatter | solution.py:277
  771.9 38.6 %reduce-scatter.23.cloned.1.call-done = f32[96,192]{1,0:T(8,128)} async-done(((f32[768,192]{1,0:T(8,128)}), f32[96,192]{1,0:T(8,128)}) %reduce-scatter.23.cloned.1.call-update) | async-done | bytes 73744 | tf_op jit(solution)/shard_map/reduce_scatter | solution.py:278
  (203 shorter events, 48.2 us)
Async XLA Ops:
  8.0 5.7 copy-start.22
  8.0 16.7 %copy-start.23 = (bf16[96,192]{1,0:T(8,128)(2,1)S(1)}, bf16[96,192]{1,0:T(8,128)(2,1)}, u32[]{:S(2)}) copy-start(bf16[96,192]{1,0:T(8,128)(2,1)} %param.38) | copy-start | bytes 110596
  8.0 44.7 %all-gather.6.cloned.1.call-start = ((), (), s32[]{:S(2)}) async-start(), calls=%async_computation.10 | async-start | bytes 1966080 | tf_op jit(solution)/shard_map/all_gather | solution.py:111
  9.3 24.9 %copy-start.29 = (f32[256]{0:T(256)}, f32[256]{0:T(256)S(1)}, u32[]{:S(2)}) copy-start(f32[256]{0:T(256)S(1)} %broadcast_multiply_fusion.8) | copy-start | bytes 3076
  10.7 23.5 %copy-start.31 = (f32[256]{0:T(256)}, f32[256]{0:T(256)S(1)}, u32[]{:S(2)}) copy-start(f32[256]{0:T(256)S(1)} %add_rsqrt_fusion.1) | copy-start | bytes 3076
  12.9 164.7 %reduce-scatter.11.cloned.1.call-start = ((), (), s32[]{:S(2)}) async-start(), calls=%async_computation.11 | async-start | bytes 3932160 | tf_op jit(solution)/shard_map/reduce_scatter | solution.py:166
  24.7 33.3 %copy-start.17 = (bf16[768,192]{1,0:T(8,128)(2,1)}, bf16[768,192]{1,0:T(8,128)(2,1)S(1)}, u32[]{:S(2)}) copy-start(bf16[768,192]{1,0:T(8,128)(2,1)S(1)} %all_gather.32) | copy-start | bytes 884740
  34.3 23.7 %copy-start.15 = (bf16[768,192]{1,0:T(8,128)(2,1)}, bf16[768,192]{1,0:T(8,128)(2,1)S(1)}, u32[]{:S(2)}) copy-start(bf16[768,192]{1,0:T(8,128)(2,1)S(1)} %all_gather.33) | copy-start | bytes 884740
  34.3 29.8 %copy-start.24 = (bf16[96,192]{1,0:T(8,128)(2,1)S(1)}, bf16[96,192]{1,0:T(8,128)(2,1)}, u32[]{:S(2)}) copy-start(bf16[96,192]{1,0:T(8,128)(2,1)} %param.35) | copy-start | bytes 110596
  34.3 48.3 %copy-start.25 = (bf16[96,192]{1,0:T(8,128)(2,1)S(1)}, bf16[96,192]{1,0:T(8,128)(2,1)}, u32[]{:S(2)}) copy-start(bf16[96,192]{1,0:T(8,128)(2,1)} %param.40) | copy-start | bytes 110596
  52.8 41.2 %copy-start.2 = (bf16[1024,768]{1,0:T(8,128)(2,1)S(1)}, bf16[1024,768]{1,0:T(8,128)(2,1)}, u32[]{:S(2)}) copy-start(bf16[1024,768]{1,0:T(8,128)(2,1)} %all-gather.6.cloned.1.call-done) | copy-start | bytes 4718596
  58.0 36.7 %collective-permute-start.1 = (bf16[2,1024,192]{1,2,0:T(8,128)(2,1)}, bf16[2,1024,192]{1,2,0:T(8,128)(2,1)}, u32[]{:S(2)}, u32[]{:S(2)}) collective-permute-start(bf16[2,1024,192]{1,2,0:T(8,128)(2,1)} %pad_maximum_fusion.1), channel_id=1, source_target_pairs={{4,0},{8,4},{12,8},{16,12},{20,16},{24,20},{28,24},{5,1},{9,5},{13... | collective-permute-start | bytes 2359304 | tf_op jit(solution)/shard_map/ppermute | solution.py:24
  59.3 35.4 %collective-permute-start = (bf16[2,1024,192]{1,2,0:T(8,128)(2,1)}, bf16[2,1024,192]{1,2,0:T(8,128)(2,1)}, u32[]{:S(2)}, u32[]{:S(2)}) collective-permute-start(bf16[2,1024,192]{1,2,0:T(8,128)(2,1)} %pad_maximum_fusion.1), channel_id=1, source_target_pairs={{0,4},{4,8},{8,12},{12,16},{16,20},{20,24},{24,28},{1,5},{5,9},{9,... | collective-permute-start | bytes 2359304 | tf_op jit(solution)/shard_map/ppermute | solution.py:23
  82.6 12.1 %copy-start.19 = (bf16[768,192]{1,0:T(8,128)(2,1)}, bf16[768,192]{1,0:T(8,128)(2,1)S(1)}, u32[]{:S(2)}) copy-start(bf16[768,192]{1,0:T(8,128)(2,1)S(1)} %all_gather.34) | copy-start | bytes 884740
  102.8 2.2 copy-start.7
  111.6 2.2 copy-start.7
  114.6 3.5 copy-start.21
  114.6 63.0 %copy-start.1 = (f32[256,768]{1,0:T(8,128)S(1)}, f32[256,768]{1,0:T(8,128)}, u32[]{:S(2)}) copy-start(f32[256,768]{1,0:T(8,128)} %param.30) | copy-start | bytes 2359300
  118.1 66.3 %all-gather.10.cloned.1.call-start = ((), (), s32[]{:S(2)}) async-start(), calls=%async_computation.13 | async-start | bytes 1327104 | tf_op jit(solution)/shard_map/all_gather | solution.py:174
  118.1 61.6 %copy-start.28 = (f32[768]{0:T(1024)S(1)}, f32[768]{0:T(1024)}, u32[]{:S(2)}) copy-start(f32[768]{0:T(1024)} %param.42) | copy-start | bytes 9220
  118.1 61.6 %copy-start.37 = (f32[768]{0:T(1024)S(1)}, f32[768]{0:T(1024)}, u32[]{:S(2)}) copy-start(f32[768]{0:T(1024)} %param.43) | copy-start | bytes 9220
  118.7 98.9 %all-gather.8.cloned.1.call-start = ((), (), s32[]{:S(2)}) async-start(), calls=%async_computation.12 | async-start | bytes 1966080 | tf_op jit(solution)/shard_map/all_gather | solution.py:172
  180.7 61.4 %all-gather.12.cloned.1.call-start = ((), (), s32[]{:S(2)}) async-start(), calls=%async_computation.14 | async-start | bytes 1327104 | tf_op jit(solution)/shard_map/all_gather | solution.py:175
  181.3 131.6 %reduce-scatter.15.cloned.1.call-start = ((), (), s32[]{:S(2)}) async-start(), calls=%async_computation.16 | async-start | bytes 3932160 | tf_op jit(solution)/shard_map/reduce_scatter | solution.py:197
  184.3 57.8 %copy-start.39 = (f32[768]{0:T(1024)S(1)}, f32[768]{0:T(1024)}, u32[]{:S(2)}) copy-start(f32[768]{0:T(1024)} %add.362) | copy-start | bytes 9220
  242.1 7.3 copy-start.41
  248.2 1.2 copy-start.42
  252.4 123.1 %reduce-scatter.13.cloned.1.call-start = ((), (), s32[]{:S(2)}) async-start(), calls=%async_computation.15 | async-start | bytes 3932160 | tf_op jit(solution)/shard_map/reduce_scatter | solution.py:183
  257.3 160.7 %all-gather.14.cloned.1.call-start = ((), (), s32[]{:S(2)}) async-start(), calls=%async_computation.17 | async-start | bytes 1966080 | tf_op jit(solution)/shard_map/all_gather | solution.py:212
  380.9 182.4 %reduce-scatter.17.cloned.1.call-start = ((), (), s32[]{:S(2)}) async-start(), calls=%async_computation.18 | async-start | bytes 3932160 | tf_op jit(solution)/shard_map/reduce_scatter | solution.py:264
  431.1 8.1 slice-start
  433.2 6.0 slice-start.1
  438.1 1.0 copy-start.10
  440.0 2.1 copy-start
  447.2 8.1 slice-start
  449.3 6.0 slice-start.1
  456.1 2.1 copy-start
  458.2 4.9 copy-start.12
  458.2 4.9 copy-start.20
  460.4 4.3 collective-permute-start.2
  461.8 6.9 collective-permute-start.3
  463.8 6.7 copy-start.18
  470.5 3.6 copy-start.13
  470.5 1.3 copy-start.16
  474.1 1.4 copy-start.40
  474.1 135.3 %reduce-scatter.27.cloned.1.call-start = ((), (), s32[]{:S(2)}) async-start(), calls=%async_computation.23 | async-start | bytes 2654208 | tf_op jit(solution)/shard_map/reduce_scatter | solution.py:201
  479.9 5.6 copy-start.9
  479.9 175.9 %reduce-scatter.29.cloned.1.call-start = ((), (), s32[]{:S(2)}) async-start(), calls=%async_computation.24 | async-start | bytes 2654208 | tf_op jit(solution)/shard_map/reduce_scatter | solution.py:202
  485.4 3.2 copy-start.3
  485.4 5.4 copy-start.38
  485.4 209.1 %reduce-scatter.25.cloned.1.call-start = ((), (), s32[]{:S(2)}) async-start(), calls=%async_computation.22 | async-start | bytes 884736 | tf_op jit(solution)/shard_map/reduce_scatter | solution.py:279
  488.5 2.9 copy-start.14
  488.5 244.7 %reduce-scatter.19.cloned.1.call-start = ((), (), s32[]{:S(2)}) async-start(), calls=%async_computation.19 | async-start | bytes 884736 | tf_op jit(solution)/shard_map/reduce_scatter | solution.py:276
  490.2 281.7 %reduce-scatter.21.cloned.1.call-start = ((), (), s32[]{:S(2)}) async-start(), calls=%async_computation.20 | async-start | bytes 884736 | tf_op jit(solution)/shard_map/reduce_scatter | solution.py:277
  493.0 113.4 %copy-start.6 = (f32[256,768]{1,0:T(8,128)S(1)}, f32[256,768]{1,0:T(8,128)}, u32[]{:S(2)}) copy-start(f32[256,768]{1,0:T(8,128)} %copy-done.5) | copy-start | bytes 2359300
  493.1 317.4 %reduce-scatter.23.cloned.1.call-start = ((), (), s32[]{:S(2)}) async-start(), calls=%async_computation.21 | async-start | bytes 884736 | tf_op jit(solution)/shard_map/reduce_scatter | solution.py:278
  494.6 68.7 %copy-start.27 = (f32[768]{0:T(1024)S(1)}, f32[768]{0:T(1024)}, u32[]{:S(2)}) copy-start(f32[768]{0:T(1024)} %param.33) | copy-start | bytes 9220
  494.6 70.2 %copy-start.26 = (f32[3072]{0:T(1024)S(1)}, f32[3072]{0:T(1024)}, u32[]{:S(2)}) copy-start(f32[3072]{0:T(1024)} %mul.315) | copy-start | bytes 36868
  494.8 68.5 %copy-start.30 = (f32[256]{0:T(256)S(1)}, f32[256]{0:T(256)}, u32[]{:S(2)}) copy-start(f32[256]{0:T(256)} %copy-done.29) | copy-start | bytes 3076
  494.8 68.5 %copy-start.32 = (f32[256]{0:T(256)S(1)}, f32[256]{0:T(256)}, u32[]{:S(2)}) copy-start(f32[256]{0:T(256)} %copy-done.31) | copy-start | bytes 3076
  494.8 70.1 %copy-start.33 = (f32[768]{0:T(1024)S(1)}, f32[768]{0:T(1024)}, u32[]{:S(2)}) copy-start(f32[768]{0:T(1024)} %get-tuple-element.567) | copy-start | bytes 9220
  494.8 70.1 %copy-start.34 = (f32[768]{0:T(1024)S(1)}, f32[768]{0:T(1024)}, u32[]{:S(2)}) copy-start(f32[768]{0:T(1024)} %get-tuple-element.573) | copy-start | bytes 9220
  494.8 70.1 %copy-start.35 = (f32[768]{0:T(1024)S(1)}, f32[768]{0:T(1024)}, u32[]{:S(2)}) copy-start(f32[768]{0:T(1024)} %get-tuple-element.620) | copy-start | bytes 9220
  494.8 70.1 %copy-start.36 = (f32[768]{0:T(1024)S(1)}, f32[768]{0:T(1024)}, u32[]{:S(2)}) copy-start(f32[768]{0:T(1024)} %get-tuple-element.636) | copy-start | bytes 9220
  (7 other events, 5.8 us)
Sparse Core Ops, SparseCore 0:
  13.0 39.7 all-gather.5
  118.2 59.3 reduce-scatter.10
  381.1 36.8 all-gather.13
  474.3 89.0 reduce-scatter.16
  567.1 42.3 reduce-scatter.26
  613.3 42.4 reduce-scatter.28
  659.5 34.9 reduce-scatter.24
  698.2 34.9 reduce-scatter.18
  736.9 34.9 reduce-scatter.20
  775.5 34.9 reduce-scatter.22
Sparse Core Ops, SparseCore 1:
  120.4 22.7 all-gather.9
  180.8 36.7 all-gather.7
  219.3 22.7 all-gather.11
  252.5 60.4 reduce-scatter.14
  315.3 60.2 reduce-scatter.12
where the time goes:
time: 820 us; the launch traced here: 818 us
  waiting for transfers between devices  553 us (67%)
  blocking collectives  92.1 us (11%)
  matrix products  79.1 us (10%)
  other arithmetic  40.3 us (5%)
  local copies, waits for them, and re-layouts  27.3 us (3%)
  between operations  16.3 us (2%)
  starting transfers between devices  9.21 us (1%)
    reduce_scatter x1, waiting for transfers between devices, on_device(): lax.psum_scatter(contract_cols(dquery, query_w) + contract_cols(dkey, key...  63.9 us
    reduce_scatter x1, waiting for transfers between devices, on_device(): lax.psum_scatter(jnp.dot(activated, w_down, preferred_element_type=f32),...  59.7 us
    reduce_scatter x1, waiting for transfers between devices, on_device(): lax.psum_scatter(contract_cols(context, out_w), 'tp', scatter_dimension=0...  58.8 us
    reduce_scatter x1, waiting for transfers between devices, on_device(): lax.psum_scatter(jnp.dot(dpreact, w_up, preferred_element_type=f32), 'tp'...  55.6 us
    reduce_scatter x1, waiting for transfers between devices, on_device(): lax.psum_scatter(grad_down_part, 'fsdp', scatter_dimension=0, tiled=True)  46.3 us
    psum x1, blocking collectives, on_device(): lax.psum((grad_gain1, grad_shift1, grad_qbias, grad_vbias, grad_obias, gr...  41.5 us
    reduce_scatter x1, waiting for transfers between devices, on_device(): lax.psum_scatter(grad_key, 'fsdp', scatter_dimension=0, tiled=True)  38.7 us
    reduce_scatter x1, waiting for transfers between devices, on_device(): lax.psum_scatter(grad_query, 'fsdp', scatter_dimension=0, tiled=True)  38.7 us
  transfers between devices with their start and end apart: 19, of which 16 were waited for; matrix products, arithmetic and copies ran while one was open for 6% of the time, Pallas kernels for 0%

commit v1 on v0

--- a/solution.py
+++ b/solution.py
@@ -3,6 +3,7 @@
 import jax.numpy as jnp
 from jax import lax
 from jax.sharding import PartitionSpec as P
+from jax.lax import axis_index, axis_size, ppermute
 
 HD = 64
 CLIP = 1536
@@ -11,6 +12,35 @@
 root_half = 0.7071067811865476
 inv_root_tau = 0.3989422804014327
 far_negative = -1e30
+
+
+def rest_the_layers_all(field, along_dim):
+    field = jnp.moveaxis(field, 0, along_dim)
+    aux = field.shape
+    w1 = field.reshape(*aux[:along_dim], aux[along_dim] * aux[along_dim + 1], *aux[along_dim + 2 :])
+    return w1
+
+
+def follow_the_frames(tile_in, axis_id, dim_no):
+    degree = axis_size(axis_id)
+    history = tuple(((nth, (nth + 1) % degree) for nth in range(degree)))
+    leaves = tuple(((no, dev_j) for dev_j, no in history))
+    spare, n_now = ([], [])
+    num = 0
+    while num < degree - 1:
+        if num % 2 == 0:
+            taken_in = ppermute(spare[-1] if spare else tile_in, axis_name=axis_id, perm=history)
+            spare.append(taken_in)
+        else:
+            n_now.append(ppermute(n_now[-1] if n_now else tile_in, axis_name=axis_id, perm=leaves))
+        num += 1
+    lower = jnp.stack([*spare[::-1], tile_in, *n_now])
+    out_arr = axis_index(axis_id)
+    tmp = len(spare)
+    inter = out_arr - tmp
+    lower = lower[(jnp.arange(degree) - inter) % degree]
+    parts_out = rest_the_layers_all(lower, dim_no)
+    return parts_out
 
 
 def extended(value, sides, width):
@@ -172,7 +202,7 @@
     normed2 = lax.all_gather(normed2_own, "tp", axis=0, tiled=True)
     w_up, w_down = (
         lax.all_gather(fc1_weight, "fsdp", axis=0, tiled=True),
-        lax.all_gather(fc2_weight, "fsdp", axis=0, tiled=True),
+        follow_the_frames(fc2_weight, "fsdp", 0),
     )
     unit_count = fc1_weight.shape[0]
     bias_up = lax.dynamic_index_in_dim(

time: 820 us -> 794 us (0.968)
  waiting for transfers between devices: 553 us -> 511 us
  local copies, waits for them, and re-layouts: 27.3 us -> 42.9 us
    all_gather x1, waiting for transfers between devices: 33.2 us -> 7 us  [on_device(): normed2 = lax.all_gather(normed2_own, 'tp', axis=0, tiled=True)]
    all_gather x1 -> x0, waiting for transfers between devices: 19.1 us -> none  [on_device(): lax.all_gather(fc2_weight, 'fsdp', axis=0, tiled=True)]
    unnamed x76 -> x85, local copies, waits for them, and re-layouts: 4.8 us -> 17.9 us
    ppermute x0 -> x7, waiting for transfers between devices: none -> 9.52 us  [the longest x4 5.44 us: follow_the_frames(): ppermute(spare[-1] if spare else tile_in, axis_name=axis_id, perm=history)]
  transfers between devices with their start and end apart: 19 -> 25, of which waited for: 16 -> 17; matrix products, arithmetic and copies ran while one was open for 6% -> 7% of each run, Pallas kernels for 0% -> 0%
where the time goes in v1:
time: 794 us; the launch traced here: 792 us
  waiting for transfers between devices  511 us (64%)
  blocking collectives  92.1 us (12%)
  matrix products  74.1 us (9%)
  local copies, waits for them, and re-layouts  42.9 us (5%)
  other arithmetic  39.6 us (5%)
  between operations  16.3 us (2%)
  starting transfers between devices  16.1 us (2%)
    reduce_scatter x1, waiting for transfers between devices, on_device(): lax.psum_scatter(contract_cols(dquery, query_w) + contract_cols(dkey, key...  64.7 us
    reduce_scatter x1, waiting for transfers between devices, on_device(): lax.psum_scatter(jnp.dot(activated, w_down, preferred_element_type=f32),...  59.7 us
    reduce_scatter x1, waiting for transfers between devices, on_device(): lax.psum_scatter(jnp.dot(dpreact, w_up, preferred_element_type=f32), 'tp'...  54.5 us
    reduce_scatter x1, waiting for transfers between devices, on_device(): lax.psum_scatter(contract_cols(context, out_w), 'tp', scatter_dimension=0...  53 us
    reduce_scatter x1, waiting for transfers between devices, on_device(): lax.psum_scatter(grad_down_part, 'fsdp', scatter_dimension=0, tiled=True)  46.3 us
    psum x1, blocking collectives, on_device(): lax.psum((grad_gain1, grad_shift1, grad_qbias, grad_vbias, grad_obias, gr...  41.5 us
    reduce_scatter x1, waiting for transfers between devices, on_device(): lax.psum_scatter(grad_key, 'fsdp', scatter_dimension=0, tiled=True)  38.7 us
    reduce_scatter x1, waiting for transfers between devices, on_device(): lax.psum_scatter(grad_out, 'fsdp', scatter_dimension=0, tiled=True)  38.7 us
  transfers between devices with their start and end apart: 25, of which 17 were waited for; matrix products, arithmetic and copies ran while one was open for 7% of the time, Pallas kernels for 0%

profile of v1, /device:TPU:0, one launch (start us, length us, event | category | flops | bytes accessed | tf_op | source)
XLA Modules:
  0.0 792.5 jit_solution(7327658905034914366)
XLA Ops:
  10.7 2.1 add_convert_fusion.2
  13.7 11.0 %all_gather.29 = bf16[768,192]{1,0:T(8,128)(2,1)S(1)} all-gather(bf16[96,192]{1,0:T(8,128)(2,1)S(1)} %copy-done.23), channel_id=1, replica_groups=mesh['fsdp'=8,'tp'=4] {'fsdp'}, dimensions={0}, use_global_device_ids=true | all-gather | bytes 331776 | tf_op jit(solution)/shard_map/all_gather | solution.py:102
  24.7 9.5 %all_gather.30 = bf16[768,192]{1,0:T(8,128)(2,1)S(1)} all-gather(bf16[96,192]{1,0:T(8,128)(2,1)S(1)} %copy-done.24), channel_id=1, replica_groups=mesh['fsdp'=8,'tp'=4] {'fsdp'}, dimensions={0}, use_global_device_ids=true | all-gather | bytes 331776 | tf_op jit(solution)/shard_map/all_gather | solution.py:103
  34.3 18.5 %all-gather.5.cloned.1.call-done = bf16[1024,768]{1,0:T(8,128)(2,1)} async-done(((bf16[256,768]{1,0:T(8,128)(2,1)}), bf16[1024,768]{1,0:T(8,128)(2,1)}) %all-gather.5.cloned.1.call-update) | async-done | bytes 1572880 | tf_op jit(solution)/shard_map/all_gather | solution.py:141
  52.8 2.2 fusion.27
  57.9 4.0 collective-permute-start
  62.7 18.6 %all_gather.31 = bf16[768,192]{1,0:T(8,128)(2,1)S(1)} all-gather(bf16[96,192]{1,0:T(8,128)(2,1)S(1)} %copy-done.25), channel_id=1, replica_groups=mesh['fsdp'=8,'tp'=4] {'fsdp'}, dimensions={0}, use_global_device_ids=true | all-gather | bytes 331776 | tf_op jit(solution)/shard_map/all_gather | solution.py:101
  81.2 11.4 %all_gather.32 = bf16[768,192]{1,0:T(8,128)(2,1)} all-gather(bf16[96,192]{1,0:T(8,128)(2,1)S(1)} %copy-done.26), channel_id=1, replica_groups=mesh['fsdp'=8,'tp'=4] {'fsdp'}, dimensions={0}, use_global_device_ids=true | all-gather | bytes 331776 | tf_op jit(solution)/shard_map/all_gather | solution.py:104
  95.7 17.6 %while.40 = (s32[]{:T(128)}, bf16[1024,192]{0,1:T(8,128)(2,1)}, f32[3,1024]{1,0:T(4,128)S(1)}, s32[]{:T(128)}, bf16[2,3072,192]{1,2,0:T(8,128)(2,1)S(1)}, /*inde...) while((s32[]{:T(128)}, bf16[1024,192]{0,1:T(8,128)(2,1)}, ...), condition=%wide.region_6.7_spmd.clone, body=%wide.region_2.6_spmd.clone.sunk | while | flops 630030336 | bytes 36239832 | solution.py:190
  99.3 2.1 exponential_reduce_fusion.2
  101.5 2.2 fusion.117
  108.1 2.1 exponential_reduce_fusion.2
  110.2 2.2 fusion.117
  113.3 3.4 fusion.42
  117.7 5.4 collective-permute-done.2
  123.2 53.0 %reduce-scatter.11.cloned.1.call-done = f32[256,768]{1,0:T(8,128)} async-done(((f32[1024,768]{1,0:T(8,128)}), f32[256,768]{1,0:T(8,128)}) %reduce-scatter.11.cloned.1.call-update) | async-done | bytes 786448 | tf_op jit(solution)/shard_map/reduce_scatter | solution.py:196
  180.9 4.1 collective-permute-done.6
  185.0 2.8 collective-permute-start.7
  191.8 2.6 collective-permute-start.8
  194.4 1.6 bitcast_dynamic-update-slice_fusion.7
  196.0 1.6 bitcast_dynamic-update-slice_fusion.6
  197.6 1.6 bitcast_dynamic-update-slice_fusion.5
  199.2 1.6 bitcast_dynamic-update-slice_fusion.4
  200.8 1.6 bitcast_dynamic-update-slice_fusion.3
  202.3 1.6 bitcast_dynamic-update-slice_fusion.2
  203.9 1.6 bitcast_dynamic-update-slice_fusion.1
  206.2 3.0 gather_fusion
  209.2 7.0 all-gather.7.cloned.1.call-done
  216.2 4.7 multiply_convert_fusion.1
  220.9 2.9 convert_reduce_fusion
  225.0 3.0 fusion.44
  228.1 4.8 fusion.43
  233.0 54.5 %reduce-scatter.15.cloned.1.call-done = f32[256,768]{1,0:T(8,128)} async-done(((f32[1024,768]{1,0:T(8,128)}), f32[256,768]{1,0:T(8,128)}) %reduce-scatter.15.cloned.1.call-update) | async-done | bytes 786448 | tf_op jit(solution)/shard_map/reduce_scatter | solution.py:227
  287.5 2.4 multiply_reduce_fusion
  290.5 59.7 %reduce-scatter.13.cloned.1.call-done = f32[256,768]{1,0:T(8,128)} async-done(((f32[1024,768]{1,0:T(8,128)}), f32[256,768]{1,0:T(8,128)}) %reduce-scatter.13.cloned.1.call-update) | async-done | bytes 786448 | tf_op jit(solution)/shard_map/reduce_scatter | solution.py:213
  350.1 3.7 fusion.37
  355.6 37.0 %all-gather.11.cloned.1.call-done = bf16[1024,768]{1,0:T(8,128)(2,1)} async-done(((bf16[256,768]{1,0:T(8,128)(2,1)}), bf16[1024,768]{1,0:T(8,128)(2,1)}) %all-gather.11.cloned.1.call-update) | async-done | bytes 1572880 | tf_op jit(solution)/shard_map/all_gather | solution.py:242
  392.5 3.3 convert_multiply_fusion
  397.8 2.7 broadcast_in_dim.132
  400.5 32.3 %while.41 = (s32[]{:T(128)}, bf16[1024,192]{0,1:T(8,128)(2,1)}, f32[2,3072,192]{1,2,0:T(8,128)}, s32[]{:T(128)}, bf16[2,3072,192]{1,2,0:T(8,128)(2,1)S(1)}, /*in...) while((s32[]{:T(128)}, bf16[1024,192]{0,1:T(8,128)(2,1)}, ...), condition=%wide.region_17.18_spmd.clone, body=%wide.region_15.17_spmd.clone.sunk | while | flops 1537181184 | bytes 94420032 | solution.py:276
  405.6 2.1 fusion.130
  407.7 3.4 multiply_convert_fusion.3
  414.5 2.1 copy-done
  421.8 2.1 fusion.130
  423.9 3.4 multiply_convert_fusion.3
  430.6 2.1 copy-done
  432.8 2.2 fusion.39
  439.3 4.0 collective-permute-done.10
  443.3 1.8 add_convert_fusion
  446.3 2.3 add_add_fusion
  450.0 4.3 fusion.48
  455.8 4.7 fusion.29
  461.5 2.9 fusion.47
  464.5 1.6 fusion.46
  466.2 2.5 fusion.32
  470.5 2.6 fusion.34
  473.1 64.7 %reduce-scatter.17.cloned.1.call-done = f32[256,768]{1,0:T(8,128)} async-done(((f32[1024,768]{1,0:T(8,128)}), f32[256,768]{1,0:T(8,128)}) %reduce-scatter.17.cloned.1.call-update) | async-done | bytes 786448 | tf_op jit(solution)/shard_map/reduce_scatter | solution.py:294
  539.4 41.5 %all-reduce = (f32[768]{0:T(1024)}, f32[768]{0:T(1024)}, f32[768]{0:T(1024)}, f32[768]{0:T(1024)}, f32[768]{0:T(1024)}, /*index=5*/f32[768]{0:T(1024)}, f32[768]{0:T(1024)}, f32[3072]{0:T(1024)}, f32[768]{0:T(1024)}) all-reduce(f32[768]{0:T(1024)S(1)} %get-tuple-element.569, ...), channel_id=1, replica_groups=mesh['fsdp'=8,'tp'=4] {'fsdp','tp'}, use_global_device_ids=true, to_apply=%region_22.23 | all-reduce | flops 9216 | bytes 73728 | tf_op jit(solution)/shard_map/psum | solution.py:321
  581.0 2.3 multiply_add_fusion
  584.0 46.3 %reduce-scatter.29.cloned.1.call-done = f32[96,768]{1,0:T(8,128)} async-done(((f32[768,768]{1,0:T(8,128)}), f32[96,768]{1,0:T(8,128)}) %reduce-scatter.29.cloned.1.call-update) | async-done | bytes 294928 | tf_op jit(solution)/shard_map/reduce_scatter | solution.py:232
  630.3 38.7 %reduce-scatter.25.cloned.1.call-done = f32[96,192]{1,0:T(8,128)} async-done(((f32[768,192]{1,0:T(8,128)}), f32[96,192]{1,0:T(8,128)}) %reduce-scatter.25.cloned.1.call-update) | async-done | bytes 73744 | tf_op jit(solution)/shard_map/reduce_scatter | solution.py:309
  669.0 38.7 %reduce-scatter.19.cloned.1.call-done = f32[96,192]{1,0:T(8,128)} async-done(((f32[768,192]{1,0:T(8,128)}), f32[96,192]{1,0:T(8,128)}) %reduce-scatter.19.cloned.1.call-update) | async-done | bytes 73744 | tf_op jit(solution)/shard_map/reduce_scatter | solution.py:306
  707.7 38.7 %reduce-scatter.21.cloned.1.call-done = f32[96,192]{1,0:T(8,128)} async-done(((f32[768,192]{1,0:T(8,128)}), f32[96,192]{1,0:T(8,128)}) %reduce-scatter.21.cloned.1.call-update) | async-done | bytes 73744 | tf_op jit(solution)/shard_map/reduce_scatter | solution.py:307
  746.4 38.5 %reduce-scatter.23.cloned.1.call-done = f32[96,192]{1,0:T(8,128)} async-done(((f32[768,192]{1,0:T(8,128)}), f32[96,192]{1,0:T(8,128)}) %reduce-scatter.23.cloned.1.call-update) | async-done | bytes 73744 | tf_op jit(solution)/shard_map/reduce_scatter | solution.py:308
  (227 shorter events, 65.4 us)
Async XLA Ops:
  8.0 5.7 copy-start.23
  8.0 16.7 %copy-start.24 = (bf16[96,192]{1,0:T(8,128)(2,1)S(1)}, bf16[96,192]{1,0:T(8,128)(2,1)}, u32[]{:S(2)}) copy-start(bf16[96,192]{1,0:T(8,128)(2,1)} %param.38) | copy-start | bytes 110596
  8.0 44.7 %all-gather.5.cloned.1.call-start = ((), (), s32[]{:S(2)}) async-start(), calls=%async_computation.10 | async-start | bytes 1966080 | tf_op jit(solution)/shard_map/all_gather | solution.py:141
  9.3 24.9 %copy-start.29 = (f32[256]{0:T(256)}, f32[256]{0:T(256)S(1)}, u32[]{:S(2)}) copy-start(f32[256]{0:T(256)S(1)} %broadcast_multiply_fusion.8) | copy-start | bytes 3076
  10.7 23.5 %copy-start.31 = (f32[256]{0:T(256)}, f32[256]{0:T(256)S(1)}, u32[]{:S(2)}) copy-start(f32[256]{0:T(256)S(1)} %add_rsqrt_fusion.1) | copy-start | bytes 3076
  12.9 163.3 %reduce-scatter.11.cloned.1.call-start = ((), (), s32[]{:S(2)}) async-start(), calls=%async_computation.11 | async-start | bytes 3932160 | tf_op jit(solution)/shard_map/reduce_scatter | solution.py:196
  24.7 31.0 %copy-start.16 = (bf16[768,192]{1,0:T(8,128)(2,1)}, bf16[768,192]{1,0:T(8,128)(2,1)S(1)}, u32[]{:S(2)}) copy-start(bf16[768,192]{1,0:T(8,128)(2,1)S(1)} %all_gather.29) | copy-start | bytes 884740
  34.3 21.4 %copy-start.14 = (bf16[768,192]{1,0:T(8,128)(2,1)}, bf16[768,192]{1,0:T(8,128)(2,1)S(1)}, u32[]{:S(2)}) copy-start(bf16[768,192]{1,0:T(8,128)(2,1)S(1)} %all_gather.30) | copy-start | bytes 884740
  52.8 2.2 copy-start.2
  55.0 7.7 copy-start.25
  55.0 26.2 %copy-start.26 = (bf16[96,192]{1,0:T(8,128)(2,1)S(1)}, bf16[96,192]{1,0:T(8,128)(2,1)}, u32[]{:S(2)}) copy-start(bf16[96,192]{1,0:T(8,128)(2,1)} %param.40) | copy-start | bytes 110596
  56.6 36.7 %collective-permute-start.1 = (bf16[2,1024,192]{1,2,0:T(8,128)(2,1)}, bf16[2,1024,192]{1,2,0:T(8,128)(2,1)}, u32[]{:S(2)}, u32[]{:S(2)}) collective-permute-start(bf16[2,1024,192]{1,2,0:T(8,128)(2,1)} %pad_maximum_fusion.1), channel_id=1, source_target_pairs={{4,0},{8,4},{12,8},{16,12},{20,16},{24,20},{28,24},{5,1},{9,5},{13... | collective-permute-start | bytes 2359304 | tf_op jit(solution)/shard_map/ppermute | solution.py:54
  57.9 35.4 %collective-permute-start = (bf16[2,1024,192]{1,2,0:T(8,128)(2,1)}, bf16[2,1024,192]{1,2,0:T(8,128)(2,1)}, u32[]{:S(2)}, u32[]{:S(2)}) collective-permute-start(bf16[2,1024,192]{1,2,0:T(8,128)(2,1)} %pad_maximum_fusion.1), channel_id=1, source_target_pairs={{0,4},{4,8},{8,12},{12,16},{16,20},{20,24},{24,28},{1,5},{5,9},{9,... | collective-permute-start | bytes 2359304 | tf_op jit(solution)/shard_map/ppermute | solution.py:53
  81.2 12.1 %copy-start.18 = (bf16[768,192]{1,0:T(8,128)(2,1)}, bf16[768,192]{1,0:T(8,128)(2,1)S(1)}, u32[]{:S(2)}) copy-start(bf16[768,192]{1,0:T(8,128)(2,1)S(1)} %all_gather.31) | copy-start | bytes 884740
  101.4 2.2 copy-start.7
  110.2 2.2 copy-start.7
  113.3 3.4 copy-start.21
  116.7 59.5 %copy-start.1 = (f32[256,768]{1,0:T(8,128)S(1)}, f32[256,768]{1,0:T(8,128)}, u32[]{:S(2)}) copy-start(f32[256,768]{1,0:T(8,128)} %param.30) | copy-start | bytes 2359300
  116.7 92.5 %all-gather.9.cloned.1.call-start = ((), (), s32[]{:S(2)}) async-start(), calls=%async_computation.13 | async-start | bytes 1327104 | tf_op jit(solution)/shard_map/all_gather | solution.py:204
  116.7 61.6 %copy-start.28 = (f32[768]{0:T(1024)S(1)}, f32[768]{0:T(1024)}, u32[]{:S(2)}) copy-start(f32[768]{0:T(1024)} %param.42) | copy-start | bytes 9220
  116.8 61.6 %copy-start.37 = (f32[768]{0:T(1024)S(1)}, f32[768]{0:T(1024)}, u32[]{:S(2)}) copy-start(f32[768]{0:T(1024)} %param.43) | copy-start | bytes 9220
  117.3 98.9 %all-gather.7.cloned.1.call-start = ((), (), s32[]{:S(2)}) async-start(), calls=%async_computation.12 | async-start | bytes 1966080 | tf_op jit(solution)/shard_map/all_gather | solution.py:202
  117.3 5.8 collective-permute-start.2
  123.2 57.7 %collective-permute-start.3 = (bf16[96,768]{1,0:T(8,128)(2,1)}, bf16[96,768]{1,0:T(8,128)(2,1)}, u32[]{:S(2)}, u32[]{:S(2)}) collective-permute-start(bf16[96,768]{1,0:T(8,128)(2,1)} %collective-permute-done.2), channel_id=1, source_target_pairs={{0,4},{4,8},{8,12},{12,16},{16,20},{20,24},{24,28},{28,0},{1,5},{5... | collective-permute-start | bytes 442376 | tf_op jit(solution)/shard_map/ppermute | solution.py:32
  179.4 108.2 %reduce-scatter.15.cloned.1.call-start = ((), (), s32[]{:S(2)}) async-start(), calls=%async_computation.15 | async-start | bytes 3932160 | tf_op jit(solution)/shard_map/reduce_scatter | solution.py:227
  179.4 5.6 collective-permute-start.6
  180.9 6.9 collective-permute-start.4
  185.0 6.8 collective-permute-start.7
  187.8 6.6 collective-permute-start.5
  191.8 13.8 %collective-permute-start.8 = (bf16[96,768]{1,0:T(8,128)(2,1)}, bf16[96,768]{1,0:T(8,128)(2,1)S(1)}, u32[]{:S(2)}, u32[]{:S(2)}) collective-permute-start(bf16[96,768]{1,0:T(8,128)(2,1)} %collective-permute-done.7), channel_id=1, source_target_pairs={{4,0},{8,4},{12,8},{16,12},{20,16},{24,20},{28,24},{0,28},{5,1},{9... | collective-permute-start | bytes 442376 | tf_op jit(solution)/shard_map/ppermute | solution.py:35
  209.2 11.7 %copy-start.39 = (f32[768]{0:T(1024)S(1)}, f32[768]{0:T(1024)}, u32[]{:S(2)}) copy-start(f32[768]{0:T(1024)} %add.386) | copy-start | bytes 9220
  216.2 4.7 copy-start.20
  216.2 4.7 copy-start.22
  220.9 4.1 copy-start.41
  228.1 122.0 %reduce-scatter.13.cloned.1.call-start = ((), (), s32[]{:S(2)}) async-start(), calls=%async_computation.14 | async-start | bytes 3932160 | tf_op jit(solution)/shard_map/reduce_scatter | solution.py:213
  233.0 159.5 %all-gather.11.cloned.1.call-start = ((), (), s32[]{:S(2)}) async-start(), calls=%async_computation.16 | async-start | bytes 1966080 | tf_op jit(solution)/shard_map/all_gather | solution.py:242
  355.5 182.3 %reduce-scatter.17.cloned.1.call-start = ((), (), s32[]{:S(2)}) async-start(), calls=%async_computation.17 | async-start | bytes 3932160 | tf_op jit(solution)/shard_map/reduce_scatter | solution.py:294
  405.6 8.1 %slice-start = ((s8[4718592]{0:T(1024)(128)(4,1)}), s8[4194304]{0:T(1024)(128)(4,1)S(1)}, s32[]{:S(2)}) async-start(s8[4718592]{0:T(1024)(128)(4,1)} %bitcast.147), calls=%async_computation.24 | async-start | bytes 8388608 | tf_op jit(solution)/shard_map/while
  407.7 6.0 slice-start.1
  414.5 2.1 copy-start
  421.8 8.1 %slice-start = ((s8[4718592]{0:T(1024)(128)(4,1)}), s8[4194304]{0:T(1024)(128)(4,1)S(1)}, s32[]{:S(2)}) async-start(s8[4718592]{0:T(1024)(128)(4,1)} %bitcast.147), calls=%async_computation.24 | async-start | bytes 8388608 | tf_op jit(solution)/shard_map/while
  423.9 6.0 slice-start.1
  430.6 2.1 copy-start
  432.8 4.9 copy-start.12
  432.8 4.9 copy-start.19
  435.0 4.3 collective-permute-start.9
  436.4 6.9 collective-permute-start.10
  438.3 6.7 copy-start.17
  445.1 3.6 copy-start.13
  448.7 135.3 %reduce-scatter.27.cloned.1.call-start = ((), (), s32[]{:S(2)}) async-start(), calls=%async_computation.22 | async-start | bytes 2654208 | tf_op jit(solution)/shard_map/reduce_scatter | solution.py:231
  454.4 175.9 %reduce-scatter.29.cloned.1.call-start = ((), (), s32[]{:S(2)}) async-start(), calls=%async_computation.23 | async-start | bytes 2654208 | tf_op jit(solution)/shard_map/reduce_scatter | solution.py:232
  460.5 3.9 copy-start.3
  460.5 208.5 %reduce-scatter.25.cloned.1.call-start = ((), (), s32[]{:S(2)}) async-start(), calls=%async_computation.21 | async-start | bytes 884736 | tf_op jit(solution)/shard_map/reduce_scatter | solution.py:309
  464.4 243.3 %reduce-scatter.19.cloned.1.call-start = ((), (), s32[]{:S(2)}) async-start(), calls=%async_computation.18 | async-start | bytes 884736 | tf_op jit(solution)/shard_map/reduce_scatter | solution.py:306
  466.1 280.3 %reduce-scatter.21.cloned.1.call-start = ((), (), s32[]{:S(2)}) async-start(), calls=%async_computation.19 | async-start | bytes 884736 | tf_op jit(solution)/shard_map/reduce_scatter | solution.py:307
  468.8 69.1 %copy-start.27 = (f32[768]{0:T(1024)S(1)}, f32[768]{0:T(1024)}, u32[]{:S(2)}) copy-start(f32[768]{0:T(1024)} %param.33) | copy-start | bytes 9220
  468.8 69.1 %copy-start.30 = (f32[256]{0:T(256)S(1)}, f32[256]{0:T(256)}, u32[]{:S(2)}) copy-start(f32[256]{0:T(256)} %copy-done.29) | copy-start | bytes 3076
  468.8 69.1 %copy-start.32 = (f32[256]{0:T(256)S(1)}, f32[256]{0:T(256)}, u32[]{:S(2)}) copy-start(f32[256]{0:T(256)} %copy-done.31) | copy-start | bytes 3076
  468.8 316.1 %reduce-scatter.23.cloned.1.call-start = ((), (), s32[]{:S(2)}) async-start(), calls=%async_computation.20 | async-start | bytes 884736 | tf_op jit(solution)/shard_map/reduce_scatter | solution.py:308
  470.5 68.9 %copy-start.33 = (f32[768]{0:T(1024)S(1)}, f32[768]{0:T(1024)}, u32[]{:S(2)}) copy-start(f32[768]{0:T(1024)} %get-tuple-element.567) | copy-start | bytes 9220
  470.5 68.9 %copy-start.34 = (f32[768]{0:T(1024)S(1)}, f32[768]{0:T(1024)}, u32[]{:S(2)}) copy-start(f32[768]{0:T(1024)} %get-tuple-element.573) | copy-start | bytes 9220
  470.5 68.9 %copy-start.35 = (f32[768]{0:T(1024)S(1)}, f32[768]{0:T(1024)}, u32[]{:S(2)}) copy-start(f32[768]{0:T(1024)} %get-tuple-element.620) | copy-start | bytes 9220
  470.5 68.9 %copy-start.36 = (f32[768]{0:T(1024)S(1)}, f32[768]{0:T(1024)}, u32[]{:S(2)}) copy-start(f32[768]{0:T(1024)} %get-tuple-element.636) | copy-start | bytes 9220
  470.5 110.5 %copy-start.6 = (f32[256,768]{1,0:T(8,128)S(1)}, f32[256,768]{1,0:T(8,128)}, u32[]{:S(2)}) copy-start(f32[256,768]{1,0:T(8,128)} %copy-done.5) | copy-start | bytes 2359300
  (14 other events, 14.8 us)
Sparse Core Ops, SparseCore 0:
  13.0 39.7 all-gather.4
  116.8 59.3 reduce-scatter.10
  355.6 36.8 all-gather.10
  448.8 89.0 reduce-scatter.16
  541.6 42.3 reduce-scatter.26
  587.8 42.4 reduce-scatter.28
  634.0 34.9 reduce-scatter.24
  672.7 34.9 reduce-scatter.18
  711.4 34.9 reduce-scatter.20
  749.9 34.9 reduce-scatter.22
Sparse Core Ops, SparseCore 1:
  119.1 22.7 all-gather.8
  179.4 36.7 all-gather.6
  228.2 59.3 reduce-scatter.14
  289.8 60.2 reduce-scatter.12
